TPU v7x, 32 devices: a whole 2x2x4 slice. The times are simulated.
32 devices in a mesh: grid: 32 (over z, y, x, core).
Axes of the slice: x: 2, y: 2, z: 4, core: 2. Of those that a mesh axis runs over, the one named last changes fastest.
Arguments:
- right_sides: float32 [32, 32, 48, 128], P(None, 'grid'), may hold values from -54 to 54, as said below
- recycle: float32 [2, 24, 32, 48, 128], P(None, None, 'grid'), may hold values from -6 to 6
- medium: float32 [32, 48, 128], P('grid'), may hold values from 0.05 to 1
- shift_table: float32 [8], replicated, may hold values from 0.25 to 2
- shift_index: int32 [2], replicated, may hold values from 0 to 7
Outputs:
- solution: float32 [32, 32, 48, 128], P(None, 'grid')
- residue: float32 [32, 32, 48, 128], P(None, 'grid')
Inputs may be any that keep to these rules, and one draw needn't show every extreme that they name: `right_sides`: finite real values.
All inputs are finite; a program needn't handle non-finite values.
Results may differ from a plain program's by a relative error of at most 0.0003.
Values sent between devices are 32-bit elements; how exact they have to be, the bound alone decides.
A program may use at most 64 MiB of HBM per device.

v0:
```python
import functools

import jax
import jax.numpy as jnp
from jax import lax
from jax.experimental import pallas as pl
from jax.experimental.pallas import tpu as pltpu
from jax.sharding import PartitionSpec as P

STEPS = 3
LANES = 128
MESH = pl.DeviceIdType.MESH
highest = lax.Precision.HIGHEST


def dot(left, right):
    return lax.dot_general(
        left, right, (((1,), (0,)), ((), ())), precision=highest, preferred_element_type=jnp.float32
    )


def dot_t(left, right):
    return lax.dot_general(
        left, right, (((1,), (1,)), ((), ())), precision=highest, preferred_element_type=jnp.float32
    )


def iota2(shape, dim):
    return lax.broadcasted_iota(jnp.int32, shape, dim)


def eye(size):
    return jnp.where(iota2((size, size), 0) == iota2((size, size), 1), 1.0, 0.0)


def factor_all(matrices, count):
    size = matrices[0].shape[0]
    rows = iota2((size, 1), 0)
    unit = jnp.where(rows < count, eye(size), 0.0)
    parts = [(m, unit) for m in matrices]
    for k in range(count):
        fresh = []
        for a, z in parts:
            scale = 1.0 / a[k : k + 1, k : k + 1]
            f = jnp.where(rows > k, a[:, k : k + 1] * scale, 0.0)
            fresh.append((a - f * a[k : k + 1, :], z - f * z[k : k + 1, :]))
        parts = fresh
    upper = iota2((size, size), 1) >= iota2((size, size), 0)
    out = []
    for a, z in parts:
        pivots = jnp.sum(a * unit, axis=1, keepdims=True)
        root = jnp.where(rows < count, lax.rsqrt(jnp.where(rows < count, pivots, 1.0)), 0.0)
        out.append((jnp.where(upper, a * root, 0.0), z * root))
    return out


def solve_all(matrices, rights):
    size = matrices[0].shape[0]
    rows = iota2((size, 1), 0)
    unit = eye(size)
    parts = list(zip(matrices, rights))
    for k in range(size):
        fresh = []
        for a, r in parts:
            scale = 1.0 / a[k : k + 1, k : k + 1]
            f = jnp.where(rows == k, 0.0, a[:, k : k + 1] * scale)
            fresh.append((a - f * a[k : k + 1, :], r - f * r[k : k + 1, :]))
        parts = fresh
    return [r / jnp.sum(a * unit, axis=1, keepdims=True) for a, r in parts]


def kernel(
    n, factors, chunk,
    u_ref, b_ref, med_ref, table_ref, index_ref, sol_ref, res_ref,
    space, halo_u, halo_v, gram0, gram, coef, hbt, ebt, fin, back,
    send_sem, recv_sem, red_send, red_recv,
):
    me = lax.axis_index("grid")
    k_rows = u_ref.shape[1]
    block = b_ref.shape[1]
    cells = b_ref.shape[2]
    count = cells // chunk
    pad = space.shape[1] - (STEPS + 1) * block
    left, right = me - 1, me + 1
    has = (me > 0, me < n - 1)

    barrier = pltpu.get_barrier_semaphore()
    peers = []
    stride = 1
    for f in factors:
        mine = lax.rem(me // stride, f)
        base = me - mine * stride
        peers.append((f, stride, mine, base))
        stride *= f
    total = 0
    for f, stride, mine, base in peers:
        for d in range(1, f):
            pl.semaphore_signal(
                barrier, inc=1, device_id=(base + lax.rem(mine + d, f) * stride,), device_id_type=MESH
            )
            total += 1
    for to in (lax.rem(me + n - 1, n), lax.rem(me + 1, n)):
        pl.semaphore_signal(barrier, inc=1, device_id=(to,), device_id_type=MESH)
    pl.semaphore_wait(barrier, total + 2)

    def halo_copy(stage, side, i):
        inner = pl.ds(pl.multiple_of(i * chunk, LANES), chunk)
        outer = pl.ds(pl.multiple_of(i * chunk + LANES, LANES), chunk)
        if stage == 0:
            src, dst = u_ref.at[:, :, outer], halo_u.at[side, :, :, inner]
        else:
            src = space.at[:, pl.ds(pad + block * (stage - 1), block), outer]
            dst = halo_v.at[stage - 1, side, :, :, inner]
        return pltpu.make_async_remote_copy(
            src_ref=src, dst_ref=dst,
            send_sem=send_sem.at[stage, side, i], recv_sem=recv_sem.at[stage, side, i],
            device_id=((left, right)[side],), device_id_type=MESH,
        )

    def halo_start(stage, i):
        for side in range(2):
            @pl.when(has[side])
            def _():
                halo_copy(stage, side, i).start()

    def halo_wait(stage, i):
        for side in range(2):
            @pl.when(has[1 - side])
            def _():
                halo_copy(stage, side, i).wait_recv()

    def reduce_sum(buffer, number, values):
        offset = 0
        for f, stride, mine, base in peers:
            own = offset + mine
            for g in range(2):
                buffer[number, own, g, :, :] = values[g]
            for d in range(1, f):
                to = lax.rem(mine + d, f)
                pltpu.make_async_remote_copy(
                    src_ref=buffer.at[number, own], dst_ref=buffer.at[number, own],
                    send_sem=red_send.at[number if buffer is gram0 else number + 1, offset + d],
                    recv_sem=red_recv.at[number if buffer is gram0 else number + 1, own],
                    device_id=(base + to * stride,), device_id_type=MESH,
                ).start()
            for d in range(1, f):
                there = lax.rem(mine + d, f)
                origin = offset + there
                pltpu.make_async_remote_copy(
                    src_ref=buffer.at[number, origin], dst_ref=buffer.at[number, origin],
                    send_sem=red_send.at[number if buffer is gram0 else number + 1, offset + d],
                    recv_sem=red_recv.at[number if buffer is gram0 else number + 1, origin],
                    device_id=(base + there * stride,), device_id_type=MESH,
                ).wait_recv()
            values = []
            for g in range(2):
                value = buffer[number, offset, g, :, :]
                for s in range(1, f):
                    value = value + buffer[number, offset + s, g, :, :]
                values.append(value)
            offset += f
        return values

    def reduce_drain(buffer, number):
        offset = 0
        for f, stride, mine, base in peers:
            for d in range(1, f):
                pltpu.make_async_remote_copy(
                    src_ref=buffer.at[number, offset + mine], dst_ref=buffer.at[number, offset + mine],
                    send_sem=red_send.at[number if buffer is gram0 else number + 1, offset + d],
                    recv_sem=red_recv.at[number if buffer is gram0 else number + 1, offset + mine],
                    device_id=(base + lax.rem(mine + d, f) * stride,), device_id_type=MESH,
                ).wait_send()
            offset += f

    def send_loop(i, carry):
        halo_start(0, i)
        return carry

    lax.fori_loop(0, count, send_loop, 0)

    shifts = []
    for g in range(2):
        shift = jnp.float32(0.0)
        for s in range(table_ref.shape[0]):
            shift = shift + jnp.where(index_ref[g] == s, table_ref[s], 0.0)
        shifts.append(6.0 + shift)

    zero_rows = space.shape[1]
    for g in range(2):
        space[g, :, 0:LANES] = jnp.zeros((zero_rows, LANES), jnp.float32)
        space[g, :, cells + LANES : cells + 2 * LANES] = jnp.zeros((zero_rows, LANES), jnp.float32)
        if pad > k_rows:
            space[g, k_rows:pad, :] = jnp.zeros((pad - k_rows, space.shape[2]), jnp.float32)
    for side in range(2):
        @pl.when(jnp.logical_not(has[1 - side]))
        def _():
            halo_u[side] = jnp.zeros(halo_u.shape[1:], jnp.float32)
            for j in range(STEPS):
                halo_v[j, side] = jnp.zeros(halo_v.shape[2:], jnp.float32)

    lane = iota2((1, LANES), 1)

    def stencil(load, side0, side1, g, start):
        outer = start + LANES
        c = load(outer)
        near = load(outer - LANES) + load(outer + LANES)
        near = near + side0 + side1
        near = near + jnp.where(lane == 0, 0.0, pltpu.roll(c, 1, 1))
        near = near + jnp.where(lane == LANES - 1, 0.0, pltpu.roll(c, LANES - 1, 1))
        diag = med_ref[:, pl.ds(start, LANES)] + shifts[g]
        return diag * c - near

    def first_chunk(i, carry):
        halo_wait(0, i)
        out = []
        for g in range(2):
            for q in range(chunk // LANES):
                start = pl.multiple_of(i * chunk + q * LANES, LANES)
                here = pl.ds(start, LANES)
                applied = stencil(
                    lambda at: u_ref[g, :, pl.ds(pl.multiple_of(at, LANES), LANES)],
                    halo_u[0, g, :, here], halo_u[1, g, :, here], g, start,
                )
                there = pl.ds(pl.multiple_of(start + LANES, LANES), LANES)
                space[g, 0:k_rows, there] = applied
                space[g, pad : pad + block, there] = b_ref[g, :, here]
            outer = pl.ds(pl.multiple_of(i * chunk + LANES, LANES), chunk)
            rows = space[g, 0 : pad + block, outer]
            out.append(carry[g] + dot_t(rows, rows))
        return tuple(out)

    size = pad + block
    zero = jnp.zeros((size, size), jnp.float32)
    sums = lax.fori_loop(0, count, first_chunk, (zero, zero))
    filler = jnp.zeros((size, LANES), jnp.float32)
    for g in range(2):
        fin[g, 0:size, :] = filler
        fin[g, 0:size, 0:size] = sums[g]
    sums = reduce_sum(gram0, 0, [fin[g, 0:size, :] for g in range(2)])
    for g in range(2):
        fin[g, 0:size, :] = sums[g]
    linv = [z for _, z in factor_all([fin[g, 0:pad, 0:pad] for g in range(2)], k_rows)]
    proj_t = [dot_t(fin[g, pad:size, 0:pad], linv[g]) for g in range(2)]
    remaining = [fin[g, pad:size, pad:size] - dot_t(proj_t[g], proj_t[g]) for g in range(2)]
    first_factor = factor_all(remaining, block)
    for g in range(2):
        inv = first_factor[g][1]
        coef[g, :, 0:pad] = -dot(inv, dot(proj_t[g], linv[g]))
        coef[g, :, pad:size] = inv
        hbt[g, :, :] = jnp.zeros(hbt.shape[1:], jnp.float32)

    unit = eye(block)
    for j in range(1, STEPS + 1):
        known = pad + block * j

        def combine_chunk(i, carry):
            outer = pl.ds(pl.multiple_of(i * chunk + LANES, LANES), chunk)
            for g in range(2):
                space[g, known - block : known, outer] = dot(
                    coef[g, :, 0:known], space[g, 0:known, outer]
                )
            halo_start(j, i)
            return carry

        lax.fori_loop(0, count, combine_chunk, 0)

        def gram_chunk(i, carry):
            halo_wait(j, i)
            out = []
            for g in range(2):
                for q in range(chunk // LANES):
                    start = pl.multiple_of(i * chunk + q * LANES, LANES)
                    here = pl.ds(start, LANES)
                    space[g, known : known + block, pl.ds(pl.multiple_of(start + LANES, LANES), LANES)] = stencil(
                        lambda at: space[g, known - block : known, pl.ds(pl.multiple_of(at, LANES), LANES)],
                        halo_v[j - 1, 0, g, :, here], halo_v[j - 1, 1, g, :, here], g, start,
                    )
                outer = pl.ds(pl.multiple_of(i * chunk + LANES, LANES), chunk)
                rows = space[g, 0 : known + block, outer]
                out.append(carry[g] + dot_t(rows[known:, :], rows))
            return tuple(out)

        zero = jnp.zeros((block, known + block), jnp.float32)
        sums = lax.fori_loop(0, count, gram_chunk, (zero, zero))
        for g in range(2):
            fin[g, 0:block, 0 : known + block] = sums[g]
        sums = reduce_sum(gram, j - 1, [fin[g, 0:block, :] for g in range(2)])
        for g in range(2):
            fin[g, 0:block, :] = sums[g]
        et = [dot_t(fin[g, 0:block, 0:pad], linv[g]) for g in range(2)]
        ht = [fin[g, 0:block, pad:known] for g in range(2)]
        fresh = [
            fin[g, 0:block, known : known + block] - dot_t(et[g], et[g]) - dot_t(ht[g], ht[g])
            for g in range(2)
        ]
        parts = factor_all(fresh, block)
        for g in range(2):
            lt, inv = parts[g]
            coef[g, :, 0:pad] = -dot(inv, dot(et[g], linv[g]))
            coef[g, :, pad:known] = -dot(inv, ht[g])
            coef[g, :, known : known + block] = inv
            at = block * (j - 1)
            hbt[g, at : at + block, 0 : known - pad] = ht[g]
            hbt[g, at : at + block, known - pad : known - pad + block] = dot_t(unit, lt)
            ebt[g, at : at + block, :] = et[g]

    width = pad + block * (STEPS + 1)
    kry = block * STEPS
    normal, rights = [], []
    for g in range(2):
        h = hbt[g, :, 0 : kry + block]
        normal.append(dot_t(h, h))
        rights.append(dot(hbt[g, :, 0:block], first_factor[g][0]))
    ys = solve_all(normal, rights)
    for g in range(2):
        yt = dot_t(unit, ys[g])
        back[g, :, :] = dot(proj_t[g] - dot(yt, ebt[g, :, :]), linv[g])
        rest = -dot(yt, hbt[g, :, :])
        fin[g, 0:block, :] = rest
        fin[g, 0:block, 0:block] = fin[g, 0:block, 0:block] + dot_t(unit, first_factor[g][0])
        top = fin[g, 0:block, 0:kry]
        last = dot(fin[g, 0:block, kry : kry + block], coef[g, :, 0:width])
        fin[g, 0 : 2 * block, :] = jnp.zeros((2 * block, LANES), jnp.float32)
        fin[g, 0:block, pad : pad + kry] = yt
        fin[g, block : 2 * block, 0:width] = last
        fin[g, block : 2 * block, pad : pad + kry] = fin[g, block : 2 * block, pad : pad + kry] + top

    def final_chunk(i, carry):
        outer = pl.ds(pl.multiple_of(i * chunk + LANES, LANES), chunk)
        inner = pl.ds(pl.multiple_of(i * chunk, LANES), chunk)
        for g in range(2):
            both = dot(fin[g, 0 : 2 * block, 0:width], space[g, 0:width, outer])
            sol_ref[g, :, inner] = both[0:block] + dot(back[g, :, 0:k_rows], u_ref[g, :, outer])
            res_ref[g, :, inner] = both[block:]
        return carry

    lax.fori_loop(0, count, final_chunk, 0)

    for stage in range(STEPS + 1):
        def drain(i, carry):
            for side in range(2):
                @pl.when(has[side])
                def _():
                    halo_copy(stage, side, i).wait_send()
            return carry

        lax.fori_loop(0, count, drain, 0)
    reduce_drain(gram0, 0)
    for j in range(STEPS):
        reduce_drain(gram, j)


def split_count(n):
    out = []
    while n > 1:
        f = next(f for f in (8, 4, 2, n) if n % f == 0)
        out.append(f)
        n //= f
    return out


def solution(mesh):
    n = mesh.shape["grid"]
    factors = split_count(n)

    def on_device(right_sides, recycle, medium, shift_table, shift_index):
        block = right_sides.shape[0] // 2
        k_rows = recycle.shape[1]
        cells = right_sides.shape[2] * right_sides.shape[3]
        pad = -(-k_rows // block) * block
        tiles = cells // LANES
        chunk = LANES * next(t for t in (6, 4, 3, 2, 1) if tiles % t == 0)
        count = cells // chunk
        width = pad + block * (STEPS + 1)
        b = right_sides.reshape(2, block, cells)
        u = jnp.pad(recycle.reshape(2, k_rows, cells), ((0, 0), (0, 0), (LANES, LANES)))
        slots = sum(factors)
        vmem = pl.BlockSpec(memory_space=pltpu.VMEM)
        smem = pl.BlockSpec(memory_space=pltpu.SMEM)
        shape = jax.ShapeDtypeStruct((2, block, cells), jnp.float32)
        f32 = jnp.float32
        sol, res = pl.pallas_call(
            functools.partial(kernel, n, factors, chunk),
            out_shape=(shape, shape),
            in_specs=[vmem, vmem, vmem, smem, smem],
            out_specs=(vmem, vmem),
            scratch_shapes=[
                pltpu.VMEM((2, width, cells + 2 * LANES), f32),
                pltpu.VMEM((2, 2, k_rows, cells), f32),
                pltpu.VMEM((STEPS, 2, 2, block, cells), f32),
                pltpu.VMEM((1, slots, 2, pad + block, LANES), f32),
                pltpu.VMEM((STEPS, slots, 2, block, LANES), f32),
                pltpu.VMEM((2, block, LANES), f32),
                pltpu.VMEM((2, block * STEPS, LANES), f32),
                pltpu.VMEM((2, block * STEPS, pad), f32),
                pltpu.VMEM((2, pad + block, LANES), f32),
                pltpu.VMEM((2, block, pad), f32),
                pltpu.SemaphoreType.DMA((STEPS + 1, 2, count)),
                pltpu.SemaphoreType.DMA((STEPS + 1, 2, count)),
                pltpu.SemaphoreType.DMA((STEPS + 1, slots)),
                pltpu.SemaphoreType.DMA((STEPS + 1, slots)),
            ],
            compiler_params=pltpu.CompilerParams(
                collective_id=0, has_side_effects=True, vmem_limit_bytes=48 * 1024 * 1024
            ),
        )(u, b, medium.reshape(1, cells), shift_table, shift_index)
        return sol.reshape(right_sides.shape), res.reshape(right_sides.shape)

    rows = P(None, "grid", None, None)
    return jax.shard_map(
        on_device,
        mesh=mesh,
        in_specs=(rows, P(None, None, "grid", None, None), P("grid", None, None), P(), P()),
        out_specs=(rows, rows),
        check_vma=False,
    )
```

profile of v0, /device:TPU:0, one launch (start us, length us, event | category | flops | bytes accessed | tf_op | source)
XLA Modules:
  0.0 155.9 jit_solution(6089451495042731035)
XLA Ops:
  0.6 0.0 copy-start.3
  0.6 1.4 reshape.20.b_ref
  2.0 0.1 copy-done.3
  2.1 0.2 reshape.19
  2.3 0.0 copy-start
  2.3 0.0 copy-start.1
  2.3 0.0 copy-start.2
  2.4 0.1 pad.4.u_ref
  2.4 0.6 copy-done
  3.1 0.0 copy-done.1
  3.1 0.0 copy-done.2
  3.1 150.8 %shard_map.68 = (f32[2,16,6144]{2,1,0:T(8,128)S(1)}, f32[2,16,6144]{2,1,0:T(8,128)S(1)}) custom-call(f32[2,24,6400]{2,1,0:T(8,128)S(1)} %pad.4.u_ref, f32[2,16,6144]{2,1,0:T(8,128)S(1)} %reshape.20.b_ref, f32[1,6144]{1,0:T(1,128)S(1)} %bitcast.21, f32[8]{0:T(128)S(1)} %copy-done.1, s32[2]{0:T(128)S(1)} %copy-done.2), custom_call_target="tpu_custom_call" | custom-call | tf_op jit(solution)/shard_map/pallas_call | solution.py:383
  153.8 1.0 copy.9
  154.9 1.0 copy.10
Async XLA Ops:
  0.6 1.5 copy-start.3
  2.3 0.7 copy-start
  2.3 0.7 copy-start.1
  2.3 0.7 copy-start.2
where the time goes:
time: 156 us
  Pallas kernels  151 us (97%)
  local copies, waits for them, and re-layouts  4.43 us (3%)
    pallas_call x1, Pallas kernels, on_device(): pl.pallas_call(functools.partial(kernel, n, factors, chunk), out_shape=(s...  151 us

commit v1 on v0

--- a/solution.py
+++ b/solution.py
@@ -25,12 +25,37 @@
     )
 
 
+def halves(x):
+    high = x.astype(jnp.bfloat16)
+    return high, (x - high.astype(jnp.float32)).astype(jnp.bfloat16)
+
+
+def dot_three(left, right):
+    a, b = halves(left), halves(right)
+    one = lambda p, q: jnp.dot(p, q, preferred_element_type=jnp.float32)
+    return one(a[0], b[0]) + (one(a[0], b[1]) + one(a[1], b[0]))
+
+
 def iota2(shape, dim):
     return lax.broadcasted_iota(jnp.int32, shape, dim)
 
 
 def eye(size):
     return jnp.where(iota2((size, size), 0) == iota2((size, size), 1), 1.0, 0.0)
+
+
+def pair_step(arrays, k, first, second):
+    c1, c2 = arrays[0][:, k : k + 1], arrays[0][:, k + 1 : k + 2]
+    f1 = jnp.where(first, c1 * (1.0 / c1[k : k + 1]), 0.0)
+    c2 = c2 - f1 * c2[k : k + 1]
+    f2 = jnp.where(second, c2 * (1.0 / c2[k + 1 : k + 2]), 0.0)
+    link = f1[k + 1 : k + 2]
+    out = []
+    for x in arrays:
+        r1 = x[k : k + 1, :]
+        r2 = x[k + 1 : k + 2, :] - link * r1
+        out.append(x - f1 * r1 - f2 * r2)
+    return tuple(out)
 
 
 def factor_all(matrices, count):
@@ -38,13 +63,8 @@
     rows = iota2((size, 1), 0)
     unit = jnp.where(rows < count, eye(size), 0.0)
     parts = [(m, unit) for m in matrices]
-    for k in range(count):
-        fresh = []
-        for a, z in parts:
-            scale = 1.0 / a[k : k + 1, k : k + 1]
-            f = jnp.where(rows > k, a[:, k : k + 1] * scale, 0.0)
-            fresh.append((a - f * a[k : k + 1, :], z - f * z[k : k + 1, :]))
-        parts = fresh
+    for k in range(0, count, 2):
+        parts = [pair_step(p, k, rows > k, rows > k + 1) for p in parts]
     upper = iota2((size, size), 1) >= iota2((size, size), 0)
     out = []
     for a, z in parts:
@@ -59,13 +79,8 @@
     rows = iota2((size, 1), 0)
     unit = eye(size)
     parts = list(zip(matrices, rights))
-    for k in range(size):
-        fresh = []
-        for a, r in parts:
-            scale = 1.0 / a[k : k + 1, k : k + 1]
-            f = jnp.where(rows == k, 0.0, a[:, k : k + 1] * scale)
-            fresh.append((a - f * a[k : k + 1, :], r - f * r[k : k + 1, :]))
-        parts = fresh
+    for k in range(0, size, 2):
+        parts = [pair_step(p, k, rows != k, rows != k + 1) for p in parts]
     return [r / jnp.sum(a * unit, axis=1, keepdims=True) for a, r in parts]
 
 
@@ -133,7 +148,7 @@
         offset = 0
         for f, stride, mine, base in peers:
             own = offset + mine
-            for g in range(2):
+            for g in range(len(values)):
                 buffer[number, own, g, :, :] = values[g]
             for d in range(1, f):
                 to = lax.rem(mine + d, f)
@@ -152,8 +167,9 @@
                     recv_sem=red_recv.at[number if buffer is gram0 else number + 1, origin],
                     device_id=(base + there * stride,), device_id_type=MESH,
                 ).wait_recv()
+            held = len(values)
             values = []
-            for g in range(2):
+            for g in range(held):
                 value = buffer[number, offset, g, :, :]
                 for s in range(1, f):
                     value = value + buffer[number, offset + s, g, :, :]
@@ -233,13 +249,12 @@
     size = pad + block
     zero = jnp.zeros((size, size), jnp.float32)
     sums = lax.fori_loop(0, count, first_chunk, (zero, zero))
-    filler = jnp.zeros((size, LANES), jnp.float32)
-    for g in range(2):
-        fin[g, 0:size, :] = filler
-        fin[g, 0:size, 0:size] = sums[g]
-    sums = reduce_sum(gram0, 0, [fin[g, 0:size, :] for g in range(2)])
-    for g in range(2):
-        fin[g, 0:size, :] = sums[g]
+    half = LANES // 2
+    fin[0, 0:size, :] = jnp.zeros((size, LANES), jnp.float32)
+    for g in range(2):
+        fin[0, 0:size, half * g : half * g + size] = sums[g]
+    fin[0, 0:size, :] = reduce_sum(gram0, 0, [fin[0, 0:size, :]])[0]
+    fin[1, 0:size, 0:size] = fin[0, 0:size, half : half + size]
     linv = [z for _, z in factor_all([fin[g, 0:pad, 0:pad] for g in range(2)], k_rows)]
     proj_t = [dot_t(fin[g, pad:size, 0:pad], linv[g]) for g in range(2)]
     remaining = [fin[g, pad:size, pad:size] - dot_t(proj_t[g], proj_t[g]) for g in range(2)]
@@ -330,8 +345,8 @@
         outer = pl.ds(pl.multiple_of(i * chunk + LANES, LANES), chunk)
         inner = pl.ds(pl.multiple_of(i * chunk, LANES), chunk)
         for g in range(2):
-            both = dot(fin[g, 0 : 2 * block, 0:width], space[g, 0:width, outer])
-            sol_ref[g, :, inner] = both[0:block] + dot(back[g, :, 0:k_rows], u_ref[g, :, outer])
+            both = dot_three(fin[g, 0 : 2 * block, 0:width], space[g, 0:width, outer])
+            sol_ref[g, :, inner] = both[0:block] + dot_three(back[g, :, 0:k_rows], u_ref[g, :, outer])
             res_ref[g, :, inner] = both[block:]
         return carry
 
@@ -389,7 +404,7 @@
                 pltpu.VMEM((2, width, cells + 2 * LANES), f32),
                 pltpu.VMEM((2, 2, k_rows, cells), f32),
                 pltpu.VMEM((STEPS, 2, 2, block, cells), f32),
-                pltpu.VMEM((1, slots, 2, pad + block, LANES), f32),
+                pltpu.VMEM((1, slots, 1, pad + block, LANES), f32),
                 pltpu.VMEM((STEPS, slots, 2, block, LANES), f32),
                 pltpu.VMEM((2, block, LANES), f32),
                 pltpu.VMEM((2, block * STEPS, LANES), f32),

time: 156 us -> 155 us (level)
  Pallas kernels: 151 us -> 149 us
where the time goes in v1:
time: 155 us; the launch traced here: 154 us
  Pallas kernels  149 us (96%)
  local copies, waits for them, and re-layouts  4.43 us (3%)
    pallas_call x1, Pallas kernels, on_device(): pl.pallas_call(functools.partial(kernel, n, factors, chunk), out_shape=(s...  149 us

profile of v1, /device:TPU:0, one launch (start us, length us, event | category | flops | bytes accessed | tf_op | source)
XLA Modules:
  0.0 154.3 jit_solution(16950569668915188116)
XLA Ops:
  0.6 0.0 copy-start.3
  0.6 1.4 reshape.20.b_ref
  2.0 0.1 copy-done.3
  2.1 0.2 reshape.19
  2.3 0.0 copy-start
  2.3 0.0 copy-start.1
  2.3 0.0 copy-start.2
  2.4 0.1 pad.4.u_ref
  2.4 0.6 copy-done
  3.1 0.0 copy-done.1
  3.1 0.0 copy-done.2
  3.1 149.2 %shard_map.68 = (f32[2,16,6144]{2,1,0:T(8,128)S(1)}, f32[2,16,6144]{2,1,0:T(8,128)S(1)}) custom-call(f32[2,24,6400]{2,1,0:T(8,128)S(1)} %pad.4.u_ref, f32[2,16,6144]{2,1,0:T(8,128)S(1)} %reshape.20.b_ref, f32[1,6144]{1,0:T(1,128)S(1)} %bitcast.21, f32[8]{0:T(128)S(1)} %copy-done.1, s32[2]{0:T(128)S(1)} %copy-done.2), custom_call_target="tpu_custom_call" | custom-call | tf_op jit(solution)/shard_map/pallas_call | solution.py:398
  152.3 1.0 copy.9
  153.3 1.0 copy.10
Async XLA Ops:
  0.6 1.5 copy-start.3
  2.3 0.7 copy-start
  2.3 0.7 copy-start.1
  2.3 0.7 copy-start.2
